TPU v7x, 32 devices: a whole 2x2x4 slice. The times are simulated.
32 devices in a mesh: dp: 1, cp: 32 (over z, y, x, core).
Axes of the slice: x: 2, y: 2, z: 4, core: 2. Of those that a mesh axis runs over, the one named last changes fastest.
Arguments:
- hidden: bfloat16 [1, 4096, 2880], P('dp', 'cp'), may hold values from -8 to 8
- norm_gain: float32 [2880], replicated, may hold values from 0.5 to 1.5
- query_weight: bfloat16 [2880, 2048], replicated, may hold values from -4 to 4
- keyval_weight: bfloat16 [2880, 512], replicated, may hold values from -1 to 1
- sink_logits: float32 [32], replicated, may hold values from -1 to 3
- document_ids: int32 [1, 4096], P('dp', 'cp'), may hold values from 0 to 15, never falling along the last dimension, each value on 1 to 1024 neighbouring positions
- block_owner: int32 [1, 32, 32], P('dp', 'cp'), may hold values from 0 to 31, each once within a row
- loss_mask: int32 [1, 4096], P('dp', 'cp'), may hold values from 0 to 1, as said below
Outputs:
- attended: bfloat16 [1, 4096, 2048], P('dp', 'cp')
- row_lse: float32 [1, 32, 4096], P('dp', None, 'cp')
- token_weight: float32 [1, 4096], P('dp', 'cp')
Inputs may be any that keep to these rules, and one draw needn't show every extreme that they name: `document_ids`: in each group the ids start at 0, never fall, rise by at most one from a position to the next and end at 15; a document holds at most 1024 positions. `block_owner`: for each group and device the row of 32 entries is a permutation of 0 to 31. `loss_mask`: the last flag of each group is 1.
All inputs are finite; a program needn't handle non-finite values.
Results may differ from a plain program's by a relative error of at most 0.008.
Values may be sent and summed in bfloat16 or wider, within the bound.
A program may use at most 128 MiB of HBM per device.

v0:
```python
import math

import jax
import jax.numpy as jnp
from jax import lax
from jax.sharding import PartitionSpec as P

HEAD_DIM = 64


rope_base = 150000.0
norm_eps = 1e-05
masked_score = -1e30


def rotate(values, within):
    half_dim = values.shape[-1] // 2
    frequency = jnp.power(rope_base, -jnp.arange(half_dim, dtype=jnp.float32) / half_dim)
    angles = within.astype(jnp.float32)[:, None, None] * frequency[None, None, :]
    cosine = jnp.cos(angles)
    sine_part = jnp.sin(angles)
    first = values[..., :half_dim]
    second = values[..., half_dim:]
    return jnp.concatenate(
        [first * cosine - second * sine_part, second * cosine + first * sine_part], axis=-1
    )


def doc_within(doc_index):
    length = doc_index.shape[0]
    places = jnp.arange(length, dtype=jnp.int32)
    fresh_doc = jnp.concatenate([jnp.ones((1,), dtype=bool), doc_index[1:] != doc_index[:-1]])
    starts = lax.cummax(jnp.where(fresh_doc, places, 0), axis=0)
    return places - starts


def plain_places(first_row, key_count):
    return first_row + jnp.arange(key_count, dtype=jnp.int32)


def body(
    hidden,
    norm_gain,
    query_weight,
    keyval_weight,
    sink_logits,
    document_ids,
    block_owner,
    loss_mask,
):
    shards = lax.axis_size("cp")
    my_index = lax.axis_index("cp")
    own_rows = hidden.shape[1]
    block_rows = own_rows // shards
    head_count = sink_logits.shape[0]
    kv_width = keyval_weight.shape[1] // 2
    kv_heads = kv_width // HEAD_DIM
    group_size = head_count // kv_heads
    score_scale = HEAD_DIM ** (-0.5)
    doc_all, owner_all = (
        lax.all_gather(document_ids, "cp", axis=1, tiled=True),
        lax.all_gather(block_owner, "cp", axis=1, tiled=True),
    )
    doc_index = doc_all[0]
    owner_table = owner_all[0]
    within_all = doc_within(doc_index)
    shard_range = jnp.arange(shards, dtype=jnp.int32)
    inverse = jnp.sum(
        jnp.where(
            owner_table[:, :, None] == shard_range[None, None, :], shard_range[None, :, None], 0
        ),
        axis=1,
    )
    flag_values = loss_mask[0].astype(jnp.float32)
    token_total = lax.psum(jnp.sum(flag_values), ("dp", "cp"))
    all_tokens = float(lax.axis_size("dp") * shards * own_rows)
    token_weight = (flag_values * (all_tokens / token_total))[None]
    rows_float = hidden[0].astype(jnp.float32)
    inv_rms = lax.rsqrt(jnp.mean(rows_float * rows_float, axis=1, keepdims=True) + norm_eps)
    normed = (rows_float * inv_rms * norm_gain).astype(jnp.bfloat16)
    inner_rows = jnp.tile(jnp.arange(block_rows, dtype=jnp.int32), shards)
    my_blocks = inverse[:, my_index]
    query_place = (
        jnp.repeat(shard_range, block_rows) * own_rows
        + jnp.repeat(my_blocks, block_rows) * block_rows
        + inner_rows
    )
    send_order = inverse[my_index]
    query_place = my_index * own_rows + jnp.arange(own_rows, dtype=jnp.int32)
    own_within = lax.dynamic_slice_in_dim(within_all, my_index * own_rows, own_rows, 0)
    projected = jnp.dot(normed, query_weight, preferred_element_type=jnp.float32).reshape(
        own_rows, head_count, HEAD_DIM
    )
    queries = (
        rotate(projected, own_within).astype(jnp.bfloat16).reshape(own_rows, head_count * HEAD_DIM)
    )
    keyval = jnp.dot(normed, keyval_weight, preferred_element_type=jnp.float32)
    keys_rot = (
        rotate(keyval[:, :kv_width].reshape(own_rows, kv_heads, HEAD_DIM), own_within)
        .astype(jnp.bfloat16)
        .reshape(own_rows, kv_width)
    )
    values = keyval[:, kv_width:].astype(jnp.bfloat16)
    query_doc = doc_index[query_place]
    query_heads = queries.reshape(own_rows, kv_heads, group_size, HEAD_DIM)

    def attend_block(running, key_part, value_part, first_row):
        row_top, row_total, row_sums = running
        key_count = key_part.shape[0]
        places = plain_places(first_row, key_count)
        key_doc = doc_index[places]
        allowed = (query_doc[:, None] == key_doc[None, :]) & (
            places[None, :] <= query_place[:, None]
        )
        scores = jnp.einsum(
            "qagd,kad->agqk",
            query_heads,
            key_part.reshape(key_count, kv_heads, HEAD_DIM),
            preferred_element_type=jnp.float32,
        )
        scores = scores.reshape(head_count, own_rows, key_count) * score_scale
        scores = jnp.where(allowed[None], scores, masked_score)
        new_top = jnp.maximum(row_top, jnp.max(scores, axis=-1))
        exp_scores = jnp.exp(scores - new_top[..., None])
        shrink = jnp.exp(row_top - new_top)
        new_total = row_total * shrink + jnp.sum(exp_scores, axis=-1)
        weights = exp_scores.astype(jnp.bfloat16).reshape(kv_heads, group_size, own_rows, key_count)
        mixed_values = jnp.einsum(
            "agqk,kad->agqd",
            weights,
            value_part.reshape(key_count, kv_heads, HEAD_DIM),
            preferred_element_type=jnp.float32,
        )
        mixed_values = mixed_values.reshape(head_count, own_rows, HEAD_DIM)
        return (new_top, new_total, row_sums * shrink[..., None] + mixed_values)

    initial = (
        jnp.broadcast_to(sink_logits[:, None], (head_count, own_rows)),
        jnp.ones((head_count, own_rows), jnp.float32),
        jnp.zeros((head_count, own_rows, HEAD_DIM), jnp.float32),
    )
    key_piece = lax.all_gather(keys_rot, "cp", axis=0, tiled=True)
    value_piece = lax.all_gather(values, "cp", axis=0, tiled=True)
    key_count = key_piece.shape[0]
    sub_rows = math.gcd(key_count, max(512, own_rows))

    def one_step(step_index, carried):
        offset = step_index * sub_rows
        key_part = lax.dynamic_slice_in_dim(key_piece, offset, sub_rows, 0)
        value_part = lax.dynamic_slice_in_dim(value_piece, offset, sub_rows, 0)
        return attend_block(carried, key_part, value_part, offset)

    row_top, row_total, row_sums = lax.fori_loop(0, key_count // sub_rows, one_step, initial)
    normalized = (row_sums / row_total[..., None]).astype(jnp.bfloat16)
    normalized = jnp.transpose(normalized, (1, 0, 2)).reshape(
        shards, block_rows, head_count * HEAD_DIM
    )
    log_total = row_top + jnp.log(row_total)
    attended = normalized.reshape(1, own_rows, head_count * HEAD_DIM)
    lse_blocks = jnp.take(log_total.reshape(head_count, shards, block_rows), send_order, axis=1)
    arrived_lse = lax.all_to_all(lse_blocks, "cp", split_axis=1, concat_axis=1, tiled=True)
    row_lse = arrived_lse.reshape(1, head_count, own_rows)
    return (attended, row_lse, token_weight)


def solution(mesh):
    in_specs = (
        P("dp", "cp", None),
        P(),
        P(),
        P(),
        P(),
        P("dp", "cp"),
        P("dp", "cp", None),
        P("dp", "cp"),
    )
    out_specs = (P("dp", "cp", None), P("dp", None, "cp"), P("dp", "cp"))
    return jax.shard_map(body, mesh=mesh, in_specs=in_specs, out_specs=out_specs, check_vma=False)
```

profile of v0, /device:TPU:0, one launch (start us, length us, event | category | flops | bytes accessed | tf_op | source)
XLA Modules:
  0.0 368.8 jit_solution(14982200667218131915)
XLA Ops:
  7.2 43.6 %all_gather.12 = s32[1,4096]{1,0:T(1,128)S(1)} all-gather(s32[1,128]{1,0:T(1,128)} %param.15), channel_id=1, replica_groups=mesh['dp'=1,'cp'=32] {'cp'}, dimensions={1}, use_global_device_ids=true | all-gather | bytes 16896 | tf_op jit(solution)/shard_map/all_gather | solution.py:61
  51.7 1.5 fusion.12
  53.2 2.4 fusion.20
  57.4 1.3 convert_reduce_fusion
  58.6 37.7 %psum.7 = f32[]{:T(128)} all-reduce(f32[]{:T(128)} %convert_reduce_fusion), channel_id=1, replica_groups=mesh['dp'=1,'cp'=32] {'dp','cp'}, use_global_device_ids=true, to_apply=%region_9.10 | all-reduce | flops 1 | bytes 8 | tf_op jit(solution)/shard_map/psum | solution.py:75
  96.4 16.0 %copy.46 = bf16[2880,2048]{0,1:T(8,128)(2,1)} copy(bf16[2880,2048]{1,0:T(8,128)(2,1)} %param.12) | data formatting | bytes 23592960 | tf_op args[2]
  112.4 1.1 gather_fusion.1
  114.2 40.6 %all_gather.15 = s32[1,32,32]{2,0,1:T(1,128)S(1)} all-gather(s32[1,1,32]{2,0,1:T(1,128)S(1)} %bitcast.127), channel_id=1, replica_groups=mesh['dp'=1,'cp'=32] {'cp'}, dimensions={1}, use_global_device_ids=true | all-gather | bytes 4224 | tf_op jit(solution)/shard_map/all_gather | solution.py:62
  155.2 7.1 %fusion.18 = f32[128,32,64]{0,2,1:T(8,128)S(1)} fusion(bf16[32,64,2880]{2,1,0:T(8,128)(2,1)} %bitcast.113, bf16[1,128,2880]{1,2,0:T(8,128)(2,1)} %param.10, f32[2880]{0:T(1024)S(1)} %copy-done.2, f32[128]{0:T(128)S(1)} %add_rsqrt_fusion), kind=kOutput, calls=%fused_computation.37 | convolution fusion | flops 1511424000 | bytes 13594368 | tf_op jit(solution)/shard_map/dot_general | solution.py:91
  164.3 183.6 %while.18 = (s32[]{:T(128)}, f32[32,128]{1,0:T(8,128)S(1)}, f32[32,128]{1,0:T(8,128)S(1)}, f32[32,128,64]{1,2,0:T(8,128)}, s32[128]{0:T(128)S(1)}, /*index=5*/s3...) while((s32[]{:T(128)}, f32[32,128]{1,0:T(8,128)S(1)}, ...), condition=%wide.region_6.7_spmd.clone, body=%wide.region_3.6_spmd.clone.sunk | while | flops 560938624 | bytes 66082540 | solution.py:153
  164.3 1.0 constant_dynamic-slice_fusion.5
  165.3 3.1 gather_fusion
  168.7 5.6 %fusion.46 = (f32[4,8,128]{2,1,0:T(8,128)S(1)}, f32[4,512,128,8]{2,1,3,0:T(8,128)}) fusion(pred[128,512]{0,1:T(8,128)(4,1)S(1)} %compare_and_fusion.3, bf16[512,4,64,1]{0,2,3,1:T(8,128)(2,1)S(1)} %bitcast.114, bf16[128,4,8,64]{0,3,2,1:T(8,128)(2,1)} %get-tuple-element.409), kind=kOutput, calls=%fused_computation.8.clone.1 | convolution fusion | flops 274722816 | bytes 9256960 | tf_op jit(solution)/shard_map/while/body/eval_jaxpr/qagd,kad->agqk/dot_general | solution.py:115
  174.2 1.0 constant_dynamic-slice_fusion.6
  176.0 6.6 %fusion.48 = f32[4,8,128,64]{2,3,1,0:T(8,128)} fusion(bf16[512,4,64,1]{0,2,3,1:T(8,128)(2,1)} %bitcast.117, f32[4,512,128,8]{2,1,3,0:T(8,128)} %get-tuple-element.371, f32[4,8,128]{2,1,0:T(8,128)S(1)} %bitcast.115, pred[128,512]{0,1:T(8,128)(4,1)S(1)} %compare_and_fusion.3), kind=kOutput, calls=%fused_computation.9.clone.1 | convolution fusion | flops 276824064 | bytes 9781248 | tf_op jit(solution)/shard_map/while/body/eval_jaxpr/agqk,kad->agqd/dot_general | solution.py:128
  182.6 1.8 fusion.47
  184.4 2.5 bitcast_add_fusion.5
  186.9 1.0 constant_dynamic-slice_fusion.5
  187.9 3.1 gather_fusion
  191.3 5.6 %fusion.46 = (f32[4,8,128]{2,1,0:T(8,128)S(1)}, f32[4,512,128,8]{2,1,3,0:T(8,128)}) fusion(pred[128,512]{0,1:T(8,128)(4,1)S(1)} %compare_and_fusion.3, bf16[512,4,64,1]{0,2,3,1:T(8,128)(2,1)S(1)} %bitcast.114, bf16[128,4,8,64]{0,3,2,1:T(8,128)(2,1)} %get-tuple-element.409), kind=kOutput, calls=%fused_computation.8.clone.1 | convolution fusion | flops 274722816 | bytes 9256960 | tf_op jit(solution)/shard_map/while/body/eval_jaxpr/qagd,kad->agqk/dot_general | solution.py:115
  196.9 1.0 constant_dynamic-slice_fusion.6
  198.7 6.6 %fusion.48 = f32[4,8,128,64]{2,3,1,0:T(8,128)} fusion(bf16[512,4,64,1]{0,2,3,1:T(8,128)(2,1)} %bitcast.117, f32[4,512,128,8]{2,1,3,0:T(8,128)} %get-tuple-element.371, f32[4,8,128]{2,1,0:T(8,128)S(1)} %bitcast.115, pred[128,512]{0,1:T(8,128)(4,1)S(1)} %compare_and_fusion.3), kind=kOutput, calls=%fused_computation.9.clone.1 | convolution fusion | flops 276824064 | bytes 9781248 | tf_op jit(solution)/shard_map/while/body/eval_jaxpr/agqk,kad->agqd/dot_general | solution.py:128
  205.3 1.8 fusion.47
  207.1 2.8 bitcast_add_fusion.5
  209.9 1.0 constant_dynamic-slice_fusion.5
  210.9 3.1 gather_fusion
  214.3 5.6 %fusion.46 = (f32[4,8,128]{2,1,0:T(8,128)S(1)}, f32[4,512,128,8]{2,1,3,0:T(8,128)}) fusion(pred[128,512]{0,1:T(8,128)(4,1)S(1)} %compare_and_fusion.3, bf16[512,4,64,1]{0,2,3,1:T(8,128)(2,1)S(1)} %bitcast.114, bf16[128,4,8,64]{0,3,2,1:T(8,128)(2,1)} %get-tuple-element.409), kind=kOutput, calls=%fused_computation.8.clone.1 | convolution fusion | flops 274722816 | bytes 9256960 | tf_op jit(solution)/shard_map/while/body/eval_jaxpr/qagd,kad->agqk/dot_general | solution.py:115
  219.9 1.0 constant_dynamic-slice_fusion.6
  221.7 6.6 %fusion.48 = f32[4,8,128,64]{2,3,1,0:T(8,128)} fusion(bf16[512,4,64,1]{0,2,3,1:T(8,128)(2,1)} %bitcast.117, f32[4,512,128,8]{2,1,3,0:T(8,128)} %get-tuple-element.371, f32[4,8,128]{2,1,0:T(8,128)S(1)} %bitcast.115, pred[128,512]{0,1:T(8,128)(4,1)S(1)} %compare_and_fusion.3), kind=kOutput, calls=%fused_computation.9.clone.1 | convolution fusion | flops 276824064 | bytes 9781248 | tf_op jit(solution)/shard_map/while/body/eval_jaxpr/agqk,kad->agqd/dot_general | solution.py:128
  228.3 1.8 fusion.47
  230.1 2.8 bitcast_add_fusion.5
  232.9 1.0 constant_dynamic-slice_fusion.5
  233.9 3.1 gather_fusion
  237.3 5.6 %fusion.46 = (f32[4,8,128]{2,1,0:T(8,128)S(1)}, f32[4,512,128,8]{2,1,3,0:T(8,128)}) fusion(pred[128,512]{0,1:T(8,128)(4,1)S(1)} %compare_and_fusion.3, bf16[512,4,64,1]{0,2,3,1:T(8,128)(2,1)S(1)} %bitcast.114, bf16[128,4,8,64]{0,3,2,1:T(8,128)(2,1)} %get-tuple-element.409), kind=kOutput, calls=%fused_computation.8.clone.1 | convolution fusion | flops 274722816 | bytes 9256960 | tf_op jit(solution)/shard_map/while/body/eval_jaxpr/qagd,kad->agqk/dot_general | solution.py:115
  242.9 1.0 constant_dynamic-slice_fusion.6
  244.7 6.6 %fusion.48 = f32[4,8,128,64]{2,3,1,0:T(8,128)} fusion(bf16[512,4,64,1]{0,2,3,1:T(8,128)(2,1)} %bitcast.117, f32[4,512,128,8]{2,1,3,0:T(8,128)} %get-tuple-element.371, f32[4,8,128]{2,1,0:T(8,128)S(1)} %bitcast.115, pred[128,512]{0,1:T(8,128)(4,1)S(1)} %compare_and_fusion.3), kind=kOutput, calls=%fused_computation.9.clone.1 | convolution fusion | flops 276824064 | bytes 9781248 | tf_op jit(solution)/shard_map/while/body/eval_jaxpr/agqk,kad->agqd/dot_general | solution.py:128
  251.3 1.8 fusion.47
  253.1 2.8 bitcast_add_fusion.5
  256.9 3.1 gather_fusion
  260.3 5.6 %fusion.46 = (f32[4,8,128]{2,1,0:T(8,128)S(1)}, f32[4,512,128,8]{2,1,3,0:T(8,128)}) fusion(pred[128,512]{0,1:T(8,128)(4,1)S(1)} %compare_and_fusion.3, bf16[512,4,64,1]{0,2,3,1:T(8,128)(2,1)S(1)} %bitcast.114, bf16[128,4,8,64]{0,3,2,1:T(8,128)(2,1)} %get-tuple-element.409), kind=kOutput, calls=%fused_computation.8.clone.1 | convolution fusion | flops 274722816 | bytes 9256960 | tf_op jit(solution)/shard_map/while/body/eval_jaxpr/qagd,kad->agqk/dot_general | solution.py:115
  265.9 1.0 constant_dynamic-slice_fusion.6
  267.7 6.6 %fusion.48 = f32[4,8,128,64]{2,3,1,0:T(8,128)} fusion(bf16[512,4,64,1]{0,2,3,1:T(8,128)(2,1)} %bitcast.117, f32[4,512,128,8]{2,1,3,0:T(8,128)} %get-tuple-element.371, f32[4,8,128]{2,1,0:T(8,128)S(1)} %bitcast.115, pred[128,512]{0,1:T(8,128)(4,1)S(1)} %compare_and_fusion.3), kind=kOutput, calls=%fused_computation.9.clone.1 | convolution fusion | flops 276824064 | bytes 9781248 | tf_op jit(solution)/shard_map/while/body/eval_jaxpr/agqk,kad->agqd/dot_general | solution.py:128
  274.2 1.8 fusion.47
  276.1 2.8 bitcast_add_fusion.5
  279.9 3.1 gather_fusion
  283.3 5.6 %fusion.46 = (f32[4,8,128]{2,1,0:T(8,128)S(1)}, f32[4,512,128,8]{2,1,3,0:T(8,128)}) fusion(pred[128,512]{0,1:T(8,128)(4,1)S(1)} %compare_and_fusion.3, bf16[512,4,64,1]{0,2,3,1:T(8,128)(2,1)S(1)} %bitcast.114, bf16[128,4,8,64]{0,3,2,1:T(8,128)(2,1)} %get-tuple-element.409), kind=kOutput, calls=%fused_computation.8.clone.1 | convolution fusion | flops 274722816 | bytes 9256960 | tf_op jit(solution)/shard_map/while/body/eval_jaxpr/qagd,kad->agqk/dot_general | solution.py:115
  290.7 6.6 %fusion.48 = f32[4,8,128,64]{2,3,1,0:T(8,128)} fusion(bf16[512,4,64,1]{0,2,3,1:T(8,128)(2,1)} %bitcast.117, f32[4,512,128,8]{2,1,3,0:T(8,128)} %get-tuple-element.371, f32[4,8,128]{2,1,0:T(8,128)S(1)} %bitcast.115, pred[128,512]{0,1:T(8,128)(4,1)S(1)} %compare_and_fusion.3), kind=kOutput, calls=%fused_computation.9.clone.1 | convolution fusion | flops 276824064 | bytes 9781248 | tf_op jit(solution)/shard_map/while/body/eval_jaxpr/agqk,kad->agqd/dot_general | solution.py:128
  297.2 1.8 fusion.47
  299.1 2.8 bitcast_add_fusion.5
  302.9 3.1 gather_fusion
  306.3 5.6 %fusion.46 = (f32[4,8,128]{2,1,0:T(8,128)S(1)}, f32[4,512,128,8]{2,1,3,0:T(8,128)}) fusion(pred[128,512]{0,1:T(8,128)(4,1)S(1)} %compare_and_fusion.3, bf16[512,4,64,1]{0,2,3,1:T(8,128)(2,1)S(1)} %bitcast.114, bf16[128,4,8,64]{0,3,2,1:T(8,128)(2,1)} %get-tuple-element.409), kind=kOutput, calls=%fused_computation.8.clone.1 | convolution fusion | flops 274722816 | bytes 9256960 | tf_op jit(solution)/shard_map/while/body/eval_jaxpr/qagd,kad->agqk/dot_general | solution.py:115
  313.7 6.6 %fusion.48 = f32[4,8,128,64]{2,3,1,0:T(8,128)} fusion(bf16[512,4,64,1]{0,2,3,1:T(8,128)(2,1)} %bitcast.117, f32[4,512,128,8]{2,1,3,0:T(8,128)} %get-tuple-element.371, f32[4,8,128]{2,1,0:T(8,128)S(1)} %bitcast.115, pred[128,512]{0,1:T(8,128)(4,1)S(1)} %compare_and_fusion.3), kind=kOutput, calls=%fused_computation.9.clone.1 | convolution fusion | flops 276824064 | bytes 9781248 | tf_op jit(solution)/shard_map/while/body/eval_jaxpr/agqk,kad->agqd/dot_general | solution.py:128
  320.2 1.8 fusion.47
  322.1 2.8 bitcast_add_fusion.5
  325.9 3.1 gather_fusion
  329.3 5.6 %fusion.46 = (f32[4,8,128]{2,1,0:T(8,128)S(1)}, f32[4,512,128,8]{2,1,3,0:T(8,128)}) fusion(pred[128,512]{0,1:T(8,128)(4,1)S(1)} %compare_and_fusion.3, bf16[512,4,64,1]{0,2,3,1:T(8,128)(2,1)S(1)} %bitcast.114, bf16[128,4,8,64]{0,3,2,1:T(8,128)(2,1)} %get-tuple-element.409), kind=kOutput, calls=%fused_computation.8.clone.1 | convolution fusion | flops 274722816 | bytes 9256960 | tf_op jit(solution)/shard_map/while/body/eval_jaxpr/qagd,kad->agqk/dot_general | solution.py:115
  334.8 1.0 constant_dynamic-slice_fusion.6
  336.6 6.6 %fusion.48 = f32[4,8,128,64]{2,3,1,0:T(8,128)} fusion(bf16[512,4,64,1]{0,2,3,1:T(8,128)(2,1)} %bitcast.117, f32[4,512,128,8]{2,1,3,0:T(8,128)} %get-tuple-element.371, f32[4,8,128]{2,1,0:T(8,128)S(1)} %bitcast.115, pred[128,512]{0,1:T(8,128)(4,1)S(1)} %compare_and_fusion.3), kind=kOutput, calls=%fused_computation.9.clone.1 | convolution fusion | flops 276824064 | bytes 9781248 | tf_op jit(solution)/shard_map/while/body/eval_jaxpr/agqk,kad->agqd/dot_general | solution.py:128
  343.2 1.8 fusion.47
  345.0 2.8 bitcast_add_fusion.5
  349.4 3.5 all-to-all-start
  352.9 1.4 divide_convert_fusion
  354.3 1.0 copy.50
  355.3 4.7 %all-to-all-done = f32[32,1,128]{2,1,0:T(1,128)S(1)} async-done(((f32[32,1,128]{2,1,0:T(1,128)}), f32[32,1,128]{2,1,0:T(1,128)S(1)}, u32[]{:S(2)}, u32[]{:S(2)}) %all-to-all-start) | async-done | bytes 16416 | tf_op jit(solution)/shard_map/all_to_all | solution.py:161
  (147 shorter events, 23.0 us)
Async XLA Ops:
  7.2 46.0 %copy-start = (bf16[2880,512]{1,0:T(8,128)(2,1)S(1)}, bf16[2880,512]{1,0:T(8,128)(2,1)}, u32[]{:S(2)}) copy-start(bf16[2880,512]{1,0:T(8,128)(2,1)} %param.13) | copy-start | bytes 8847364
  7.2 156.6 %all-gather.3.cloned.1.call-start = ((), (), s32[]{:S(2)}) async-start(), calls=%async_computation.1 | async-start | bytes 2162688 | tf_op jit(solution)/shard_map/all_gather | solution.py:142
  56.6 107.6 %all-gather.5.cloned.1.call-start = ((), (), s32[]{:S(2)}) async-start(), calls=%async_computation.2 | async-start | bytes 2162688 | tf_op jit(solution)/shard_map/all_gather | solution.py:143
  96.4 17.9 %copy-start.3 = (s32[1,1,32]{2,1,0:T(1,128)S(1)}, s32[1,1,32]{2,1,0:T(1,128)}, u32[]{:S(2)}) copy-start(s32[1,1,32]{2,1,0:T(1,128)} %param.16) | copy-start | bytes 388
  96.4 58.8 %copy-start.2 = (f32[2880]{0:T(1024)S(1)}, f32[2880]{0:T(1024)}, u32[]{:S(2)}) copy-start(f32[2880]{0:T(1024)} %param.11) | copy-start | bytes 34564
  155.1 8.1 %copy-start.5 = (s32[1,128]{1,0:T(1,128)S(1)}, s32[1,128]{1,0:T(1,128)}, u32[]{:S(2)}) copy-start(s32[1,128]{1,0:T(1,128)} %param.17) | copy-start | bytes 1540
  155.1 9.1 %copy-start.4 = (f32[32]{0:T(128)S(1)}, f32[32]{0:T(128)}, u32[]{:S(2)}) copy-start(f32[32]{0:T(128)} %param.14) | copy-start | bytes 388
  176.0 6.6 %copy-start.1 = (f32[4,512,128,8]{2,1,3,0:T(8,128)S(1)}, f32[4,512,128,8]{2,1,3,0:T(8,128)}, u32[]{:S(2)}) copy-start(f32[4,512,128,8]{2,1,3,0:T(8,128)} %get-tuple-element.371) | copy-start | bytes 25165828 | tf_op jit(solution)/shard_map/while
  198.7 6.6 %copy-start.1 = (f32[4,512,128,8]{2,1,3,0:T(8,128)S(1)}, f32[4,512,128,8]{2,1,3,0:T(8,128)}, u32[]{:S(2)}) copy-start(f32[4,512,128,8]{2,1,3,0:T(8,128)} %get-tuple-element.371) | copy-start | bytes 25165828 | tf_op jit(solution)/shard_map/while
  221.7 6.6 %copy-start.1 = (f32[4,512,128,8]{2,1,3,0:T(8,128)S(1)}, f32[4,512,128,8]{2,1,3,0:T(8,128)}, u32[]{:S(2)}) copy-start(f32[4,512,128,8]{2,1,3,0:T(8,128)} %get-tuple-element.371) | copy-start | bytes 25165828 | tf_op jit(solution)/shard_map/while
  244.7 6.6 %copy-start.1 = (f32[4,512,128,8]{2,1,3,0:T(8,128)S(1)}, f32[4,512,128,8]{2,1,3,0:T(8,128)}, u32[]{:S(2)}) copy-start(f32[4,512,128,8]{2,1,3,0:T(8,128)} %get-tuple-element.371) | copy-start | bytes 25165828 | tf_op jit(solution)/shard_map/while
  267.7 6.6 %copy-start.1 = (f32[4,512,128,8]{2,1,3,0:T(8,128)S(1)}, f32[4,512,128,8]{2,1,3,0:T(8,128)}, u32[]{:S(2)}) copy-start(f32[4,512,128,8]{2,1,3,0:T(8,128)} %get-tuple-element.371) | copy-start | bytes 25165828 | tf_op jit(solution)/shard_map/while
  290.7 6.6 %copy-start.1 = (f32[4,512,128,8]{2,1,3,0:T(8,128)S(1)}, f32[4,512,128,8]{2,1,3,0:T(8,128)}, u32[]{:S(2)}) copy-start(f32[4,512,128,8]{2,1,3,0:T(8,128)} %get-tuple-element.371) | copy-start | bytes 25165828 | tf_op jit(solution)/shard_map/while
  313.7 6.6 %copy-start.1 = (f32[4,512,128,8]{2,1,3,0:T(8,128)S(1)}, f32[4,512,128,8]{2,1,3,0:T(8,128)}, u32[]{:S(2)}) copy-start(f32[4,512,128,8]{2,1,3,0:T(8,128)} %get-tuple-element.371) | copy-start | bytes 25165828 | tf_op jit(solution)/shard_map/while
  336.6 6.6 %copy-start.1 = (f32[4,512,128,8]{2,1,3,0:T(8,128)S(1)}, f32[4,512,128,8]{2,1,3,0:T(8,128)}, u32[]{:S(2)}) copy-start(f32[4,512,128,8]{2,1,3,0:T(8,128)} %get-tuple-element.371) | copy-start | bytes 25165828 | tf_op jit(solution)/shard_map/while
  349.4 10.6 %all-to-all-start = ((f32[32,1,128]{2,1,0:T(1,128)}), f32[32,1,128]{2,1,0:T(1,128)S(1)}, u32[]{:S(2)}, u32[]{:S(2)}) async-start(f32[32,1,128]{2,1,0:T(1,128)} %reshape.342), calls=%async_computation | async-start | bytes 32768 | tf_op jit(solution)/shard_map/all_to_all | solution.py:161
Sparse Core Ops, SparseCore 0:
  56.7 49.3 all-gather.2
  109.0 55.1 all-gather.4
where the time goes:
time: 371 us; the launch traced here: 369 us
  blocking collectives  122 us (33%)
  matrix products  106 us (29%)
  local copies, waits for them, and re-layouts  69.3 us (19%)
  other arithmetic  46.9 us (13%)
  between operations  14.9 us (4%)
  waiting for transfers between devices  5.25 us (1%)
    dot_general x8, matrix products, attend_block(): jnp.einsum('agqk,kad->agqd', weights, value_part.reshape(key_count, kv_he...  52.5 us
    dot_general x8, matrix products, attend_block(): jnp.einsum('qagd,kad->agqk', query_heads, key_part.reshape(key_count, kv_...  44.5 us
    all_gather x1, blocking collectives, body(): lax.all_gather(document_ids, 'cp', axis=1, tiled=True)  43.6 us
    all_gather x1, blocking collectives, body(): lax.all_gather(block_owner, 'cp', axis=1, tiled=True)  40.6 us
    psum x1, blocking collectives, body(): token_total = lax.psum(jnp.sum(flag_values), ('dp', 'cp'))  37.7 us
    gather x8, local copies, waits for them, and re-layouts, attend_block(): key_doc = doc_index[places]  25.1 us
    add x8, other arithmetic, attend_block(): return (new_top, new_total, row_sums * shrink[..., None] + mixed_values)  22.3 us
    unnamed x15, local copies, waits for them, and re-layouts  18.5 us
  transfers between devices with their start and end apart: 3, of which 2 were waited for; matrix products, arithmetic and copies ran while one was open for 8% of the time, Pallas kernels for 0%

commit v1 on v0

v1 whole, which is shorter than its diff:
```python
import functools
import math

import jax
import jax.numpy as jnp
import numpy as np
from jax import lax
from jax.experimental import pallas as pl
from jax.experimental.pallas import tpu as pltpu
from jax.sharding import PartitionSpec as P

HEAD_DIM = 64
DOC_MOST = 1024

rope_base = 150000.0
norm_eps = 1e-05
masked_score = -1e30
LANES = 128
LOG2E = math.log2(math.e)
LN2 = math.log(2.0)
MESH = pl.DeviceIdType.MESH
EXACT = lax.Precision.HIGHEST


def iota(shape, axis):
    return lax.broadcasted_iota(jnp.int32, shape, axis)


def rope_tables(shards, own_rows):
    half = HEAD_DIM // 2
    frequency = rope_base ** (-np.arange(half, dtype=np.float64) / half)
    frequency = np.tile(frequency, LANES // half)
    base = np.arange(shards, dtype=np.float64)[:, None] * own_rows * frequency
    row = np.arange(own_rows, dtype=np.float64)[:, None] * frequency
    return [np.asarray(f(x), np.float32) for x in (base, row) for f in (np.cos, np.sin)]


def kernel(
    dims,
    hidden,
    gain,
    wq_hbm,
    wkv_hbm,
    sink,
    ids,
    owner,
    flags,
    cos_base,
    sin_base,
    cos_row,
    sin_row,
    attended,
    row_lse,
    token_weight,
    wq,
    wkv,
    kv,
    idbuf,
    mkbuf,
    queries,
    bias,
    lse,
    lse_out,
    lse_in,
    w_sem,
    kv_send,
    kv_recv,
    id_send,
    id_recv,
    mk_send,
    mk_recv,
    lse_send,
    lse_recv,
):
    parts, shards, reach, heads, kv_heads = dims
    me = lax.axis_index("cp")
    part = lax.axis_index("dp")
    total = parts * shards
    place = part * shards + me
    rows = hidden.shape[1]
    group = heads // kv_heads
    width = group * HEAD_DIM
    kv_width = kv_heads * HEAD_DIM
    pairs = heads // 2
    pairs_kv = group // 2
    block_rows = rows // shards
    row_bits = block_rows.bit_length() - 1
    head_bits = heads.bit_length() - 1

    def other(off):
        target = lax.rem(place + off, total)
        return {"dp": target // shards, "cp": lax.rem(target, shards)}

    barrier = pltpu.get_barrier_semaphore()

    @pl.loop(1, total)
    def _(off):
        pl.semaphore_signal(barrier, inc=1, device_id=other(off), device_id_type=MESH)

    kv_load = pltpu.make_async_copy(wkv_hbm, wkv, w_sem.at[kv_heads])
    kv_load.start()
    q_loads = [
        pltpu.make_async_copy(wq_hbm.at[:, pl.ds(c * width, width)], wq.at[c], w_sem.at[c])
        for c in range(kv_heads)
    ]
    for load in q_loads:
        load.start()

    def kv_copy(k, target):
        return pltpu.make_async_remote_copy(
            src_ref=kv.at[reach],
            dst_ref=kv.at[reach - k],
            send_sem=kv_send.at[k - 1],
            recv_sem=kv_recv.at[k - 1],
            device_id={"cp": target},
            device_id_type=MESH,
        )

    def id_copy(k, target):
        return pltpu.make_async_remote_copy(
            src_ref=ids,
            dst_ref=idbuf.at[reach - k],
            send_sem=id_send.at[k - 1],
            recv_sem=id_recv.at[k - 1],
            device_id={"cp": target},
            device_id_type=MESH,
        )

    def mk_copy(off):
        return pltpu.make_async_remote_copy(
            src_ref=flags,
            dst_ref=mkbuf.at[off],
            send_sem=mk_send.at[off - 1],
            recv_sem=mk_recv.at[off - 1],
            device_id=other(off),
            device_id_type=MESH,
        )

    def lse_copy(off):
        target = lax.rem(me + off, shards)
        return pltpu.make_async_remote_copy(
            src_ref=lse_out.at[target],
            dst_ref=lse_in.at[me],
            send_sem=lse_send.at[off - 1],
            recv_sem=lse_recv.at[off - 1],
            device_id={"cp": target},
            device_id_type=MESH,
        )

    x = hidden[0].astype(jnp.float32)
    inv_rms = lax.rsqrt(jnp.mean(x * x, axis=1, keepdims=True) + norm_eps)
    normed = (x * inv_rms * gain[...]).astype(jnp.bfloat16)

    cb, sb = cos_base[pl.ds(me, 1), :], sin_base[pl.ds(me, 1), :]
    cr, sr = cos_row[...], sin_row[...]
    lane = iota((rows, LANES), 1)
    first_half = (lane & (HEAD_DIM - 1)) < HEAD_DIM // 2
    low = lane < HEAD_DIM
    cosine = cb * cr - sb * sr
    sine = sb * cr + cb * sr
    sine = jnp.where(first_half, -sine, sine)

    def rotate(u):
        swapped = jnp.where(
            first_half,
            pltpu.roll(u, LANES - HEAD_DIM // 2, 1),
            pltpu.roll(u, HEAD_DIM // 2, 1),
        )
        return u * cosine + swapped * sine

    kv_load.wait()
    keyval = jnp.dot(normed, wkv[...], preferred_element_type=jnp.float32)
    for c in range(kv_width // LANES):
        part_k = keyval[:, c * LANES : (c + 1) * LANES]
        kv[reach, c * LANES : (c + 1) * LANES, :] = rotate(part_k).astype(jnp.bfloat16)
        part_v = keyval[:, kv_width + c * LANES : kv_width + (c + 1) * LANES]
        kv[reach, kv_width + c * LANES : kv_width + (c + 1) * LANES, :] = part_v.T.astype(
            jnp.bfloat16
        )
    idbuf[reach] = ids[...]
    mkbuf[0] = flags[...]

    pl.semaphore_wait(barrier, total - 1)

    @pl.loop(1, reach + 1)
    def _(k):
        @pl.when(me + k < shards)
        def _():
            id_copy(k, me + k).start()
            kv_copy(k, me + k).start()

        @pl.when(me - k < 0)
        def _():
            kv[reach - k] = jnp.zeros(kv.shape[1:], kv.dtype)
            idbuf[reach - k] = jnp.full(idbuf.shape[1:], -1, jnp.int32)

    @pl.loop(1, total)
    def _(off):
        mk_copy(off).start()

    for c in range(kv_heads):
        q_loads[c].wait()
        projected = jnp.dot(normed, wq[c], preferred_element_type=jnp.float32)
        for j in range(pairs_kv):
            y = rotate(projected[:, j * LANES : (j + 1) * LANES]) * (LOG2E * HEAD_DIM**-0.5)
            yr = pltpu.roll(y, HEAD_DIM, 1)
            if c % 2 == 0:
                one, two = jnp.where(low, y, 0.0), jnp.where(low, yr, 0.0)
            else:
                one, two = jnp.where(low, 0.0, yr), jnp.where(low, 0.0, y)
            queries[c * pairs_kv + j, 0:rows, :] = one.astype(jnp.bfloat16)
            queries[c * pairs_kv + j, rows : 2 * rows, :] = two.astype(jnp.bfloat16)

    @pl.loop(1, reach + 1)
    def _(k):
        @pl.when(me - k >= 0)
        def _():
            id_copy(k, me).wait_recv()

    own_ids = jnp.broadcast_to(ids[...].astype(jnp.float32), (rows, rows))
    for slot in range(reach + 1):
        key_ids = jnp.broadcast_to(idbuf[slot].astype(jnp.float32), (rows, rows)).T
        allowed = key_ids == own_ids
        if slot == reach:
            allowed = allowed & (iota((rows, rows), 0) <= iota((rows, rows), 1))
        bias[slot * rows : (slot + 1) * rows, :] = jnp.where(allowed, 0.0, masked_score)

    @pl.loop(1, reach + 1)
    def _(k):
        @pl.when(me - k >= 0)
        def _():
            kv_copy(k, me).wait_recv()

    key_count = (reach + 1) * rows

    def attend(p):
        a = p // pairs_kv
        key_part = kv[:, pl.ds(pl.multiple_of((a // 2) * LANES, LANES), LANES), :]
        key_part = key_part.reshape(key_count, LANES)
        value_rows = pl.ds(pl.multiple_of(kv_width + a * HEAD_DIM, HEAD_DIM), HEAD_DIM)
        values_t = jnp.concatenate([kv[s, value_rows, :] for s in range(reach + 1)], axis=1)
        scores = lax.dot_general(
            key_part, queries[p], (((1,), (1,)), ((), ())), preferred_element_type=jnp.float32
        )
        shift = bias[...]
        scores = scores + jnp.concatenate([shift, shift], axis=1)
        sink_row = jnp.where(
            iota((1, 2 * rows), 1) < rows, sink[2 * p] * LOG2E, sink[2 * p + 1] * LOG2E
        )
        top = jnp.maximum(jnp.max(scores, axis=0, keepdims=True), sink_row)
        weights = jnp.exp2(scores - top)
        row_total = jnp.sum(weights, axis=0, keepdims=True) + jnp.exp2(sink_row - top)
        mixed = jnp.dot(
            values_t, weights.astype(jnp.bfloat16), preferred_element_type=jnp.float32
        )
        mixed = mixed / row_total
        both = jnp.concatenate([mixed[:, :rows], mixed[:, rows:]], axis=0)
        attended[0, :, pl.ds(pl.multiple_of(p * LANES, LANES), LANES)] = both.T.astype(
            jnp.bfloat16
        )
        log_total = top * LN2 + jnp.log(row_total)
        lse[pl.ds(2 * p, 1), :] = log_total[:, :rows]
        lse[pl.ds(2 * p + 1, 1), :] = log_total[:, rows:]

    @pl.loop(0, pairs // 2)
    def _(i):
        attend(2 * i)
        attend(2 * i + 1)

    wide = block_rows * heads
    owner_hot = (jnp.broadcast_to(owner[0], (shards, shards)) == iota((shards, shards), 0)).astype(
        jnp.float32
    )
    spread = ((iota((shards, rows), 1) >> row_bits) == iota((shards, rows), 0)).astype(jnp.float32)
    takes = jnp.dot(owner_hot, spread, preferred_element_type=jnp.float32)
    inner = iota((heads, rows), 1) & (block_rows - 1)
    lse_all = lse[...]
    stacked = jnp.concatenate(
        [jnp.where(inner == r, lse_all, 0.0) for r in range(block_rows)], axis=0
    )
    outgoing = lax.dot_general(
        takes,
        stacked,
        (((1,), (1,)), ((), ())),
        preferred_element_type=jnp.float32,
        precision=EXACT,
    )
    lse_out[...] = outgoing.reshape(shards, 1, wide)
    lse_in[pl.ds(me, 1)] = lse_out[pl.ds(me, 1)]

    @pl.loop(1, shards)
    def _(off):
        lse_copy(off).start()

    @pl.loop(1, total)
    def _(off):
        mk_copy(off).wait()

    flag_sum = jnp.sum(mkbuf[...].astype(jnp.float32), axis=0)
    token_total = jnp.sum(flag_sum, axis=1, keepdims=True)
    token_weight[...] = flags[...].astype(jnp.float32) * (float(total * rows) / token_total)

    @pl.loop(1, reach + 1)
    def _(k):
        @pl.when(me + k < shards)
        def _():
            id_copy(k, me + k).wait_send()
            kv_copy(k, me + k).wait_send()

    @pl.loop(1, shards)
    def _(off):
        lse_copy(off).wait()

    arrived = lse_in[...].reshape(shards, wide)
    spread_t = ((iota((rows, shards), 0) >> row_bits) == iota((rows, shards), 1)).astype(
        jnp.float32
    )
    placed = jnp.dot(spread_t, arrived, preferred_element_type=jnp.float32, precision=EXACT)
    keep = (iota((rows, wide), 0) & (block_rows - 1)) == (iota((rows, wide), 1) >> head_bits)
    placed = jnp.where(keep, placed, 0.0)
    pick = ((iota((heads, wide), 1) & (heads - 1)) == iota((heads, wide), 0)).astype(jnp.float32)
    row_lse[0] = lax.dot_general(
        pick, placed, (((1,), (1,)), ((), ())), preferred_element_type=jnp.float32, precision=EXACT
    )


def body(
    parts,
    shards,
    hidden,
    norm_gain,
    query_weight,
    keyval_weight,
    sink_logits,
    document_ids,
    block_owner,
    loss_mask,
):
    rows, model = hidden.shape[1:]
    heads = sink_logits.shape[0]
    kv_width = keyval_weight.shape[1] // 2
    kv_heads = kv_width // HEAD_DIM
    reach = min(-(-(DOC_MOST - 1) // rows), shards - 1)
    total = parts * shards
    wide = (rows // shards) * heads
    width = heads // kv_heads * HEAD_DIM
    tables = [jnp.asarray(t) for t in rope_tables(shards, rows)]
    vmem = pl.BlockSpec(memory_space=pltpu.VMEM)
    hbm = pl.BlockSpec(memory_space=pl.ANY)
    smem = pl.BlockSpec(memory_space=pltpu.SMEM)
    dma = pltpu.SemaphoreType.DMA
    return pl.pallas_call(
        functools.partial(kernel, (parts, shards, reach, heads, kv_heads)),
        out_shape=(
            jax.ShapeDtypeStruct((1, rows, heads * HEAD_DIM), jnp.bfloat16),
            jax.ShapeDtypeStruct((1, heads, rows), jnp.float32),
            jax.ShapeDtypeStruct((1, rows), jnp.float32),
        ),
        in_specs=[vmem, vmem, hbm, hbm, smem, vmem, vmem, vmem] + [vmem] * 4,
        out_specs=(vmem, vmem, vmem),
        scratch_shapes=[
            pltpu.VMEM((kv_heads, model, width), jnp.bfloat16),
            pltpu.VMEM((model, 2 * kv_width), jnp.bfloat16),
            pltpu.VMEM((reach + 1, 2 * kv_width, rows), jnp.bfloat16),
            pltpu.VMEM((reach + 1, 1, rows), jnp.int32),
            pltpu.VMEM((total, 1, rows), jnp.int32),
            pltpu.VMEM((heads // 2, 2 * rows, LANES), jnp.bfloat16),
            pltpu.VMEM(((reach + 1) * rows, rows), jnp.float32),
            pltpu.VMEM((heads, rows), jnp.float32),
            pltpu.VMEM((shards, 1, wide), jnp.float32),
            pltpu.VMEM((shards, 1, wide), jnp.float32),
            dma((kv_heads + 1,)),
            dma((reach,)),
            dma((reach,)),
            dma((reach,)),
            dma((reach,)),
            dma((total - 1,)),
            dma((total - 1,)),
            dma((shards - 1,)),
            dma((shards - 1,)),
        ],
        compiler_params=pltpu.CompilerParams(
            collective_id=0, has_side_effects=True, vmem_limit_bytes=60 * 1024 * 1024
        ),
    )(
        hidden,
        norm_gain.reshape(1, model),
        query_weight,
        keyval_weight,
        sink_logits,
        document_ids,
        block_owner,
        loss_mask,
        *tables,
    )


def solution(mesh):
    in_specs = (
        P("dp", "cp", None),
        P(),
        P(),
        P(),
        P(),
        P("dp", "cp"),
        P("dp", "cp", None),
        P("dp", "cp"),
    )
    out_specs = (P("dp", "cp", None), P("dp", None, "cp"), P("dp", "cp"))
    local = functools.partial(body, mesh.shape["dp"], mesh.shape["cp"])
    return jax.shard_map(local, mesh=mesh, in_specs=in_specs, out_specs=out_specs, check_vma=False)
```

time: 371 us -> 65.6 us (0.18)
  blocking collectives: 122 us -> 0 us
  matrix products: 106 us -> 0 us
  local copies, waits for them, and re-layouts: 69.3 us -> 7.92 us
  Pallas kernels: 0 us -> 56.7 us
  other arithmetic: 46.9 us -> 0 us
  between operations: 14.9 us -> 0.64 us
  waiting for transfers between devices: 5.25 us -> 0 us
    dot_general x18 -> x0, matrix products: 106 us -> none  [the longest x8 52.5 us: attend_block(): jnp.einsum('agqk,kad->agqd', weights, value_part.reshape(key_count, kv_he...]
    all_gather x2 -> x0, blocking collectives: 84.2 us -> none  [the longest x1 43.6 us: body(): lax.all_gather(document_ids, 'cp', axis=1, tiled=True)]
    pallas_call x0 -> x1, Pallas kernels: none -> 56.7 us  [body(): pl.pallas_call(functools.partial(kernel, (parts, shards, reach, heads, kv...]
    psum x1 -> x0, blocking collectives: 37.7 us -> none  [body(): token_total = lax.psum(jnp.sum(flag_values), ('dp', 'cp'))]
    gather x10 -> x0, local copies, waits for them, and re-layouts: 26.9 us -> none  [the longest x8 25.1 us: attend_block(): key_doc = doc_index[places]]
    add x33 -> x0, other arithmetic: 22.5 us -> none  [the longest x8 22.3 us: attend_block(): return (new_top, new_total, row_sums * shrink[..., None] + mixed_values)]
    dynamic_slice x24 -> x0, local copies, waits for them, and re-layouts: 22.2 us -> none  [the longest x16 14.5 us: one_step(): value_part = lax.dynamic_slice_in_dim(value_piece, offset, sub_rows, 0)]
    reduce_sum x11 -> x0, other arithmetic: 17.4 us -> none  [the longest x8 14.4 us: attend_block(): new_total = row_total * shrink + jnp.sum(exp_scores, axis=-1)]
  transfers between devices with their start and end apart: 3 -> 0, of which waited for: 2 -> 0; matrix products, arithmetic and copies ran while one was open for 8% -> 0% of each run, Pallas kernels for 0% -> 0%
where the time goes in v1:
time: 65.6 us; the launch traced here: 65.3 us
  Pallas kernels  56.7 us (86%)
  local copies, waits for them, and re-layouts  7.92 us (12%)
    pallas_call x1, Pallas kernels, body(): pl.pallas_call(functools.partial(kernel, (parts, shards, reach, heads, kv...  56.7 us
    unnamed x4, local copies, waits for them, and re-layouts  6.6 us
    reshape x1, local copies, waits for them, and re-layouts, body(): norm_gain.reshape(1, model)  1.32 us

profile of v1, /device:TPU:0, one launch (start us, length us, event | category | flops | bytes accessed | tf_op | source)
XLA Modules:
  0.0 65.3 jit_solution(2147350262856918259)
XLA Ops:
  0.6 1.3 %reshape.9.gain = f32[1,2880]{1,0:T(1,128)} reshape(f32[2880]{0:T(1024)} %param.13) | data formatting | bytes 23040 | tf_op jit(solution)/shard_map/reshape | solution.py:387
  1.9 2.3 %copy.15.hidden = bf16[1,128,2880]{2,1,0:T(8,128)(2,1)} copy(bf16[1,128,2880]{1,2,0:T(8,128)(2,1)} %param.12) | data formatting | bytes 1474560 | tf_op args[0]
  4.2 56.7 %shard_map.139 = (bf16[1,128,2048]{2,1,0:T(8,128)(2,1)}, f32[1,32,128]{2,1,0:T(8,128)}, f32[1,128]{1,0:T(1,128)}) custom-call(bf16[1,128,2880]{2,1,0:T(8,128)(2,1)} %copy.15.hidden, f32[1,2880]{1,0:T(1,128)} %reshape.9.gain, bf16[2880,2048]{1,0:T(8,128)(2,1)} %wq_hbm.1, bf16[2880,512]{1,0:T(8,128)(2,1)} %wkv_hbm.1, f32[32]{0:T(128)} %sink.1, s32[1,128]{1,0:T(1,128)} %ids.1, ...), custom_call_target="tpu_custom_call" | custom-call | tf_op jit(solution)/shard_map/pallas_call | solution.py:352
  60.9 1.9 %copy.19 = bf16[1,128,2048]{2,1,0:T(8,128)(2,1)} copy(bf16[1,128,2048]{2,1,0:T(8,128)(2,1)} %get-tuple-element.6) | data formatting | bytes 1048576
  62.8 1.3 %copy.20 = f32[1,32,128]{2,1,0:T(8,128)} copy(f32[1,32,128]{2,1,0:T(8,128)} %get-tuple-element.7) | data formatting | bytes 32768
  64.1 1.1 %copy.21 = f32[1,128]{1,0:T(1,128)} copy(f32[1,128]{1,0:T(1,128)} %get-tuple-element.8) | data formatting | bytes 1024

commit v2 on v1

--- a/solution.py
+++ b/solution.py
@@ -19,6 +19,7 @@
 LOG2E = math.log2(math.e)
 LN2 = math.log(2.0)
 MESH = pl.DeviceIdType.MESH
+RELAY_AT, HAND_AT = 1, 3
 EXACT = lax.Precision.HIGHEST
 
 
@@ -76,8 +77,7 @@
     me = lax.axis_index("cp")
     part = lax.axis_index("dp")
     total = parts * shards
-    place = part * shards + me
-    rows = hidden.shape[1]
+    rows = hidden.shape[2]
     group = heads // kv_heads
     width = group * HEAD_DIM
     kv_width = kv_heads * HEAD_DIM
@@ -87,15 +87,18 @@
     row_bits = block_rows.bit_length() - 1
     head_bits = heads.bit_length() - 1
 
-    def other(off):
-        target = lax.rem(place + off, total)
-        return {"dp": target // shards, "cp": lax.rem(target, shards)}
-
     barrier = pltpu.get_barrier_semaphore()
 
-    @pl.loop(1, total)
+    @pl.loop(1, shards)
     def _(off):
-        pl.semaphore_signal(barrier, inc=1, device_id=other(off), device_id_type=MESH)
+        pl.semaphore_signal(
+            barrier, inc=1, device_id={"cp": lax.rem(me + off, shards)}, device_id_type=MESH
+        )
+
+    for d in range(1, parts):
+        pl.semaphore_signal(
+            barrier, inc=1, device_id={"dp": lax.rem(part + d, parts)}, device_id_type=MESH
+        )
 
     kv_load = pltpu.make_async_copy(wkv_hbm, wkv, w_sem.at[kv_heads])
     kv_load.start()
@@ -106,15 +109,34 @@
     for load in q_loads:
         load.start()
 
-    def kv_copy(k, target):
+    spot = lax.rem(me, reach)
+    core = lax.rem(spot, 2)
+    chip = spot // 2
+    chips = reach // 2
+    has_before = me >= reach
+
+    def kv_copy(source, slot, send, target):
         return pltpu.make_async_remote_copy(
-            src_ref=kv.at[reach],
-            dst_ref=kv.at[reach - k],
-            send_sem=kv_send.at[k - 1],
-            recv_sem=kv_recv.at[k - 1],
+            src_ref=kv.at[source],
+            dst_ref=kv.at[slot],
+            send_sem=kv_send.at[send],
+            recv_sem=kv_recv.at[slot],
             device_id={"cp": target},
             device_id_type=MESH,
         )
+
+    def kv_arrive(slot):
+        kv_copy(slot, slot, 0, me).wait_recv()
+
+    def along(source):
+        return kv_copy(source, 0, 0, me + reach)
+
+    def across(delta, source):
+        to_chip = lax.rem(chip - delta + chips, chips)
+        return kv_copy(source, 2 * delta, delta, me - spot + 2 * to_chip + core)
+
+    def partner(j, source):
+        return kv_copy(source, 2 * j + 1, chips + j, me + 1 - 2 * core)
 
     def id_copy(k, target):
         return pltpu.make_async_remote_copy(
@@ -126,13 +148,13 @@
             device_id_type=MESH,
         )
 
-    def mk_copy(off):
+    def mk_copy(d):
         return pltpu.make_async_remote_copy(
             src_ref=flags,
-            dst_ref=mkbuf.at[off],
-            send_sem=mk_send.at[off - 1],
-            recv_sem=mk_recv.at[off - 1],
-            device_id=other(off),
+            dst_ref=mkbuf.at[d],
+            send_sem=mk_send.at[d - 1],
+            recv_sem=mk_recv.at[d - 1],
+            device_id={"dp": lax.rem(part + d, parts)},
             device_id_type=MESH,
         )
 
@@ -147,9 +169,9 @@
             device_id_type=MESH,
         )
 
-    x = hidden[0].astype(jnp.float32)
+    x = hidden[0].astype(jnp.float32).T
     inv_rms = lax.rsqrt(jnp.mean(x * x, axis=1, keepdims=True) + norm_eps)
-    normed = (x * inv_rms * gain[...]).astype(jnp.bfloat16)
+    normed = (x * inv_rms * gain[...][None, :]).astype(jnp.bfloat16)
 
     cb, sb = cos_base[pl.ds(me, 1), :], sin_base[pl.ds(me, 1), :]
     cr, sr = cos_row[...], sin_row[...]
@@ -180,25 +202,70 @@
     idbuf[reach] = ids[...]
     mkbuf[0] = flags[...]
 
-    pl.semaphore_wait(barrier, total - 1)
+    pl.semaphore_wait(barrier, shards + parts - 2)
 
     @pl.loop(1, reach + 1)
     def _(k):
         @pl.when(me + k < shards)
         def _():
             id_copy(k, me + k).start()
-            kv_copy(k, me + k).start()
 
         @pl.when(me - k < 0)
         def _():
             kv[reach - k] = jnp.zeros(kv.shape[1:], kv.dtype)
             idbuf[reach - k] = jnp.full(idbuf.shape[1:], -1, jnp.int32)
 
-    @pl.loop(1, total)
-    def _(off):
-        mk_copy(off).start()
+    for d in range(1, parts):
+        mk_copy(d).start()
+
+    @pl.when(me + reach < shards)
+    def _():
+        along(reach).start()
+
+    for delta in range(1, chips):
+
+        @pl.when(chip < delta)
+        def _():
+            across(delta, reach).start()
+
+    @pl.when(core == 0)
+    def _():
+        partner(chips - 1, reach).start()
+
+    def relay():
+        @pl.when(has_before)
+        def _():
+            kv_arrive(0)
+            for delta in range(1, chips):
+
+                @pl.when(chip >= delta)
+                def _():
+                    across(delta, 0).start()
+
+            @pl.when(core == 1)
+            def _():
+                partner(0, 0).start()
+
+    def hand_over():
+        for delta in reversed(range(1, chips)):
+
+            @pl.when(me + 2 * delta >= reach)
+            def _():
+                kv_arrive(2 * delta)
+
+                @pl.when(core == 0)
+                def _():
+                    partner(delta - 1, 2 * delta).start()
+
+                @pl.when(core == 1)
+                def _():
+                    partner(delta, 2 * delta).start()
 
     for c in range(kv_heads):
+        if c == RELAY_AT:
+            relay()
+        if c == HAND_AT:
+            hand_over()
         q_loads[c].wait()
         projected = jnp.dot(normed, wq[c], preferred_element_type=jnp.float32)
         for j in range(pairs_kv):
@@ -225,11 +292,11 @@
             allowed = allowed & (iota((rows, rows), 0) <= iota((rows, rows), 1))
         bias[slot * rows : (slot + 1) * rows, :] = jnp.where(allowed, 0.0, masked_score)
 
-    @pl.loop(1, reach + 1)
-    def _(k):
-        @pl.when(me - k >= 0)
-        def _():
-            kv_copy(k, me).wait_recv()
+    for j in range(chips):
+
+        @pl.when(me + 2 * j + 1 >= reach)
+        def _():
+            kv_arrive(2 * j + 1)
 
     key_count = (reach + 1) * rows
 
@@ -285,33 +352,48 @@
         preferred_element_type=jnp.float32,
         precision=EXACT,
     )
-    lse_out[...] = outgoing.reshape(shards, 1, wide)
+    for d in range(1, parts):
+        mk_copy(d).wait()
+    own_flags = jnp.sum(mkbuf[...].astype(jnp.float32), axis=0)
+    lse_out[:, :, 0:wide] = outgoing.reshape(shards, 1, wide)
+    lse_out[:, :, wide : wide + rows] = jnp.broadcast_to(own_flags[None], (shards, 1, rows))
     lse_in[pl.ds(me, 1)] = lse_out[pl.ds(me, 1)]
 
     @pl.loop(1, shards)
     def _(off):
         lse_copy(off).start()
 
-    @pl.loop(1, total)
-    def _(off):
-        mk_copy(off).wait()
-
-    flag_sum = jnp.sum(mkbuf[...].astype(jnp.float32), axis=0)
-    token_total = jnp.sum(flag_sum, axis=1, keepdims=True)
-    token_weight[...] = flags[...].astype(jnp.float32) * (float(total * rows) / token_total)
-
     @pl.loop(1, reach + 1)
     def _(k):
         @pl.when(me + k < shards)
         def _():
             id_copy(k, me + k).wait_send()
-            kv_copy(k, me + k).wait_send()
+
+    @pl.when(me + reach < shards)
+    def _():
+        along(reach).wait_send()
+
+    for delta in range(1, chips):
+
+        @pl.when(has_before | (chip < delta))
+        def _():
+            across(delta, reach).wait_send()
+
+    for j in range(chips):
+
+        @pl.when(me + 2 * j + 2 * (1 - core) >= reach)
+        def _():
+            partner(j, reach).wait_send()
 
     @pl.loop(1, shards)
     def _(off):
         lse_copy(off).wait()
 
-    arrived = lse_in[...].reshape(shards, wide)
+    arrived = lse_in[...].reshape(shards, wide + rows)
+    flag_sum = jnp.sum(arrived[:, wide:], axis=0, keepdims=True)
+    token_total = jnp.sum(flag_sum, axis=1, keepdims=True)
+    token_weight[...] = flags[...].astype(jnp.float32) * (float(total * rows) / token_total)
+    arrived = arrived[:, :wide]
     spread_t = ((iota((rows, shards), 0) >> row_bits) == iota((rows, shards), 1)).astype(
         jnp.float32
     )
@@ -363,19 +445,19 @@
             pltpu.VMEM((model, 2 * kv_width), jnp.bfloat16),
             pltpu.VMEM((reach + 1, 2 * kv_width, rows), jnp.bfloat16),
             pltpu.VMEM((reach + 1, 1, rows), jnp.int32),
-            pltpu.VMEM((total, 1, rows), jnp.int32),
+            pltpu.VMEM((parts, 1, rows), jnp.int32),
             pltpu.VMEM((heads // 2, 2 * rows, LANES), jnp.bfloat16),
             pltpu.VMEM(((reach + 1) * rows, rows), jnp.float32),
             pltpu.VMEM((heads, rows), jnp.float32),
-            pltpu.VMEM((shards, 1, wide), jnp.float32),
-            pltpu.VMEM((shards, 1, wide), jnp.float32),
+            pltpu.VMEM((shards, 1, wide + rows), jnp.float32),
+            pltpu.VMEM((shards, 1, wide + rows), jnp.float32),
             dma((kv_heads + 1,)),
             dma((reach,)),
             dma((reach,)),
             dma((reach,)),
             dma((reach,)),
-            dma((total - 1,)),
-            dma((total - 1,)),
+            dma((max(parts - 1, 1),)),
+            dma((max(parts - 1, 1),)),
             dma((shards - 1,)),
             dma((shards - 1,)),
         ],
@@ -383,8 +465,8 @@
             collective_id=0, has_side_effects=True, vmem_limit_bytes=60 * 1024 * 1024
         ),
     )(
-        hidden,
-        norm_gain.reshape(1, model),
+        jnp.swapaxes(hidden, 1, 2),
+        norm_gain,
         query_weight,
         keyval_weight,
         sink_logits,

time: 65.6 us -> 45.7 us (0.70)
  Pallas kernels: 56.7 us -> 40.4 us
  local copies, waits for them, and re-layouts: 7.92 us -> 4.38 us
    pallas_call x1, Pallas kernels: 56.7 us -> 40.4 us  [body(): pl.pallas_call(functools.partial(kernel, (parts, shards, reach, heads, kv...]
    unnamed x4 -> x3, local copies, waits for them, and re-layouts: 6.6 us -> 4.38 us
    reshape x1 -> x0, local copies, waits for them, and re-layouts: 1.32 us -> none  [body(): norm_gain.reshape(1, model)]
where the time goes in v2:
time: 45.7 us; the launch traced here: 45.4 us
  Pallas kernels  40.4 us (88%)
  local copies, waits for them, and re-layouts  4.38 us (10%)
  between operations  0.64 us (1%)
    pallas_call x1, Pallas kernels, body(): pl.pallas_call(functools.partial(kernel, (parts, shards, reach, heads, kv...  40.4 us
    unnamed x3, local copies, waits for them, and re-layouts  4.38 us

profile of v2, /device:TPU:0, one launch (start us, length us, event | category | flops | bytes accessed | tf_op | source)
XLA Modules:
  0.0 45.4 jit_solution(8610435615997945816)
XLA Ops:
  0.6 40.4 %shard_map.139 = (bf16[1,128,2048]{2,1,0:T(8,128)(2,1)}, f32[1,32,128]{2,1,0:T(8,128)}, f32[1,128]{1,0:T(1,128)}) custom-call(bf16[1,2880,128]{2,1,0:T(8,128)(2,1)} %bitcast.1, f32[2880]{0:T(1024)} %gain.1, bf16[2880,2048]{1,0:T(8,128)(2,1)} %wq_hbm.1, bf16[2880,512]{1,0:T(8,128)(2,1)} %wkv_hbm.1, f32[32]{0:T(128)} %sink.1, s32[1,128]{1,0:T(1,128)} %ids.1, ...), custom_call_target="tpu_custom_call" | custom-call | tf_op jit(solution)/shard_map/pallas_call | solution.py:434
  41.0 1.9 %copy.18 = bf16[1,128,2048]{2,1,0:T(8,128)(2,1)} copy(bf16[1,128,2048]{2,1,0:T(8,128)(2,1)} %get-tuple-element.6) | data formatting | bytes 1048576
  42.9 1.3 %copy.19 = f32[1,32,128]{2,1,0:T(8,128)} copy(f32[1,32,128]{2,1,0:T(8,128)} %get-tuple-element.7) | data formatting | bytes 32768
  44.2 1.2 %copy.20 = f32[1,128]{1,0:T(1,128)} copy(f32[1,128]{1,0:T(1,128)} %get-tuple-element.8) | data formatting | bytes 1024

commit v3 on v2

--- a/solution.py
+++ b/solution.py
@@ -72,6 +72,7 @@
     mk_recv,
     lse_send,
     lse_recv,
+    hid,
 ):
     parts, shards, reach, heads, kv_heads = dims
     me = lax.axis_index("cp")
@@ -101,13 +102,13 @@
         )
 
     kv_load = pltpu.make_async_copy(wkv_hbm, wkv, w_sem.at[kv_heads])
+    hid_load = pltpu.make_async_copy(hidden.at[0], hid, w_sem.at[kv_heads + 1])
+    hid_load.start()
     kv_load.start()
     q_loads = [
         pltpu.make_async_copy(wq_hbm.at[:, pl.ds(c * width, width)], wq.at[c], w_sem.at[c])
         for c in range(kv_heads)
     ]
-    for load in q_loads:
-        load.start()
 
     spot = lax.rem(me, reach)
     core = lax.rem(spot, 2)
@@ -169,7 +170,8 @@
             device_id_type=MESH,
         )
 
-    x = hidden[0].astype(jnp.float32).T
+    hid_load.wait()
+    x = hid[...].astype(jnp.float32).T
     inv_rms = lax.rsqrt(jnp.mean(x * x, axis=1, keepdims=True) + norm_eps)
     normed = (x * inv_rms * gain[...][None, :]).astype(jnp.bfloat16)
 
@@ -191,6 +193,8 @@
         return u * cosine + swapped * sine
 
     kv_load.wait()
+    for load in q_loads:
+        load.start()
     keyval = jnp.dot(normed, wkv[...], preferred_element_type=jnp.float32)
     for c in range(kv_width // LANES):
         part_k = keyval[:, c * LANES : (c + 1) * LANES]
@@ -320,7 +324,7 @@
         mixed = jnp.dot(
             values_t, weights.astype(jnp.bfloat16), preferred_element_type=jnp.float32
         )
-        mixed = mixed / row_total
+        mixed = mixed * (1.0 / row_total)
         both = jnp.concatenate([mixed[:, :rows], mixed[:, rows:]], axis=0)
         attended[0, :, pl.ds(pl.multiple_of(p * LANES, LANES), LANES)] = both.T.astype(
             jnp.bfloat16
@@ -329,10 +333,10 @@
         lse[pl.ds(2 * p, 1), :] = log_total[:, :rows]
         lse[pl.ds(2 * p + 1, 1), :] = log_total[:, rows:]
 
-    @pl.loop(0, pairs // 2)
+    @pl.loop(0, pairs // pairs_kv)
     def _(i):
-        attend(2 * i)
-        attend(2 * i + 1)
+        for j in range(pairs_kv):
+            attend(pairs_kv * i + j)
 
     wide = block_rows * heads
     owner_hot = (jnp.broadcast_to(owner[0], (shards, shards)) == iota((shards, shards), 0)).astype(
@@ -438,7 +442,7 @@
             jax.ShapeDtypeStruct((1, heads, rows), jnp.float32),
             jax.ShapeDtypeStruct((1, rows), jnp.float32),
         ),
-        in_specs=[vmem, vmem, hbm, hbm, smem, vmem, vmem, vmem] + [vmem] * 4,
+        in_specs=[hbm, vmem, hbm, hbm, smem, vmem, vmem, vmem] + [vmem] * 4,
         out_specs=(vmem, vmem, vmem),
         scratch_shapes=[
             pltpu.VMEM((kv_heads, model, width), jnp.bfloat16),
@@ -451,7 +455,7 @@
             pltpu.VMEM((heads, rows), jnp.float32),
             pltpu.VMEM((shards, 1, wide + rows), jnp.float32),
             pltpu.VMEM((shards, 1, wide + rows), jnp.float32),
-            dma((kv_heads + 1,)),
+            dma((kv_heads + 2,)),
             dma((reach,)),
             dma((reach,)),
             dma((reach,)),
@@ -460,6 +464,7 @@
             dma((max(parts - 1, 1),)),
             dma((shards - 1,)),
             dma((shards - 1,)),
+            pltpu.VMEM((model, rows), jnp.bfloat16),
         ],
         compiler_params=pltpu.CompilerParams(
             collective_id=0, has_side_effects=True, vmem_limit_bytes=60 * 1024 * 1024

time: 45.7 us -> 44.9 us (0.982)
  Pallas kernels: 40.4 us -> 39.6 us
    pallas_call x1, Pallas kernels: 40.4 us -> 39.6 us  [body(): pl.pallas_call(functools.partial(kernel, (parts, shards, reach, heads, kv...]
where the time goes in v3:
time: 44.9 us; the launch traced here: 44.6 us
  Pallas kernels  39.6 us (88%)
  local copies, waits for them, and re-layouts  4.38 us (10%)
  between operations  0.64 us (1%)
    pallas_call x1, Pallas kernels, body(): pl.pallas_call(functools.partial(kernel, (parts, shards, reach, heads, kv...  39.6 us
    unnamed x3, local copies, waits for them, and re-layouts  4.38 us

profile of v3, /device:TPU:0, one launch (start us, length us, event | category | flops | bytes accessed | tf_op | source)
XLA Modules:
  0.0 44.6 jit_solution(15821956207027804703)
XLA Ops:
  0.6 39.6 %shard_map.139 = (bf16[1,128,2048]{2,1,0:T(8,128)(2,1)}, f32[1,32,128]{2,1,0:T(8,128)}, f32[1,128]{1,0:T(1,128)}) custom-call(bf16[1,2880,128]{2,1,0:T(8,128)(2,1)} %bitcast.1, f32[2880]{0:T(1024)} %gain.1, bf16[2880,2048]{1,0:T(8,128)(2,1)} %wq_hbm.1, bf16[2880,512]{1,0:T(8,128)(2,1)} %wkv_hbm.1, f32[32]{0:T(128)} %sink.1, s32[1,128]{1,0:T(1,128)} %ids.1, ...), custom_call_target="tpu_custom_call" | custom-call | tf_op jit(solution)/shard_map/pallas_call | solution.py:438
  40.2 1.9 %copy.18 = bf16[1,128,2048]{2,1,0:T(8,128)(2,1)} copy(bf16[1,128,2048]{2,1,0:T(8,128)(2,1)} %get-tuple-element.6) | data formatting | bytes 1048576
  42.1 1.3 %copy.19 = f32[1,32,128]{2,1,0:T(8,128)} copy(f32[1,32,128]{2,1,0:T(8,128)} %get-tuple-element.7) | data formatting | bytes 32768
  43.4 1.2 %copy.20 = f32[1,128]{1,0:T(1,128)} copy(f32[1,128]{1,0:T(1,128)} %get-tuple-element.8) | data formatting | bytes 1024
